TPU v7x, 256 devices: a whole 4x4x8 slice. The times are simulated.
256 devices in a mesh: seq: 16 (over z, core), head: 16 (over x, y).
Axes of the slice: x: 4, y: 4, z: 8, core: 2. Of those that a mesh axis runs over, the one named last changes fastest.
Arguments:
- grad_output: bfloat16 [16384, 4096], P('seq', 'head'), may hold values from -6 to 6
- out_weight: bfloat16 [4096, 8192], P('seq', 'head'), may hold values from -0.0625 to 0.0625
- ssd_out: bfloat16 [16384, 8192], P('seq', 'head'), may hold values from -520 to 520
- gate: bfloat16 [16384, 8192], P('seq', 'head'), may hold values from -5 to 5
- norm_weight: float32 [8192], P('head'), may hold values from 0.5 to 1.5
- time_step: float32 [128, 16384], P('head', 'seq'), may hold values from 0.01 to 0.1
- log_decay: float32 [128, 16384], P('head', 'seq'), may hold values from -0.7 to 0
- state_in: bfloat16 [16384, 8, 128], P('seq'), may hold values from -1.796875 to 1.796875
- state_out: bfloat16 [16384, 8, 128], P('seq'), may hold values from -1.796875 to 1.796875
- skip: float32 [128], P('head'), may hold values from 0.5 to 1.5
Outputs:
- grad_x: bfloat16 [16384, 8192], P('seq', 'head')
- grad_gate: bfloat16 [16384, 8192], P('seq', 'head')
- grad_out_weight: float32 [4096, 8192], P('seq', 'head')
All inputs are finite; a program needn't handle non-finite values.
Results may differ from a plain program's by a relative error of at most 0.014.
Values may be sent and summed in bfloat16 or wider, within the bound.
A program may use at most 128 MiB of HBM per device.

v0:
```python
import math
import jax
import jax.numpy as jnp
from jax import lax
from jax.sharding import Mesh
from jax.sharding import PartitionSpec as P

HEADS = 128
GROUPS = 8
BLOCK_LEN = 256
HEAD = ("head_0", "head_1")
SEQ = ("seq_0", "seq_1")
epsilon = 1e-05


def over_axes(x, axes):
    for axis in axes:
        x = lax.psum(x, axis)
    return x


def nothing_yet(x, identity):
    return jax.tree.map(
        lambda part, zero: jnp.zeros_like(part) + jnp.asarray(zero, part.dtype), x, identity
    )


def carried_in(x, axes, combine, identity):
    before = start = nothing_yet(x, identity)
    running = x
    for axis in reversed(axes):
        size, here = (lax.axis_size(axis), lax.axis_index(axis))
        pieces = jax.tree.map(lambda part: lax.all_gather(part, axis), running)
        inside, running = (start, start)
        for k in reversed(range(size)):
            passed = k > here
            running = combine(running, jax.tree.map(lambda part: part[k], pieces))
            inside = jax.tree.map(lambda new, old: jnp.where(passed, new, old), running, inside)
        before = combine(inside, before)
    return before


def on_device(
    grad_output,
    out_weight,
    ssd_out,
    gate,
    norm_weight,
    time_step,
    log_decay,
    state_in,
    state_out,
    skip,
):
    tok_rows = ssd_out.shape[0]
    local_width = ssd_out.shape[1]
    total_width = local_width * lax.axis_size(HEAD)
    full_grad = lax.all_gather(grad_output, HEAD, axis=1, tiled=True)
    values = ssd_out.astype(jnp.float32)
    gate_values = gate.astype(jnp.float32)
    sigmoid_gate = jax.nn.sigmoid(gate_values)
    silu_gate = gate_values * sigmoid_gate
    gated_values = values * silu_gate
    local_squares = jnp.sum(gated_values * gated_values, axis=1)
    columns = full_grad
    normed_grad = jnp.dot(
        columns,
        lax.all_gather(out_weight, SEQ, axis=0, tiled=True),
        preferred_element_type=jnp.float32,
    )
    squares = over_axes(local_squares, HEAD)
    weighted = over_axes(jnp.sum(norm_weight * normed_grad * gated_values, axis=1), HEAD)
    inverse_rms = lax.rsqrt(squares[:, None] / total_width + epsilon)
    normed = (gated_values * inverse_rms * norm_weight).astype(jnp.bfloat16)
    gated_grad = (
        inverse_rms * norm_weight * normed_grad
        - gated_values * inverse_rms**3 * weighted[:, None] / total_width
    )
    grad_gate = (
        gated_grad * values * sigmoid_gate * (1.0 + gate_values * (1.0 - sigmoid_gate))
    ).astype(jnp.bfloat16)
    grad_ssd = (gated_grad * silu_gate).astype(jnp.bfloat16)
    columns = full_grad
    weight_sum = lax.psum_scatter(
        lax.dot_general(
            columns, normed, (((0,), (0,)), ((), ())), preferred_element_type=jnp.float32
        ).astype(jnp.bfloat16),
        SEQ,
        scatter_dimension=0,
        tiled=True,
    ).astype(jnp.float32)
    grad_out_weight = weight_sum * (1.0 / math.sqrt(tok_rows * lax.axis_size(SEQ)))
    heads_here = time_step.shape[0]
    head_width = local_width // heads_here
    blocks = tok_rows // BLOCK_LEN
    state_width = state_in.shape[2]
    group_count = state_in.shape[1]
    first_head = lax.axis_index(HEAD) * heads_here
    head_ids = first_head + jnp.arange(heads_here, dtype=jnp.int32)
    group_ids = head_ids // (HEADS // GROUPS)
    group_pick = (group_ids[:, None] == jnp.arange(group_count, dtype=jnp.int32)[None, :]).astype(
        jnp.bfloat16
    )
    b_heads = jnp.einsum(
        "tgn,hg->htn", state_in, group_pick, preferred_element_type=jnp.float32
    ).astype(jnp.bfloat16)
    b_heads = b_heads.reshape(heads_here, blocks, BLOCK_LEN, state_width)
    c_heads = jnp.einsum(
        "tgn,hg->htn", state_out, group_pick, preferred_element_type=jnp.float32
    ).astype(jnp.bfloat16)
    c_heads = c_heads.reshape(heads_here, blocks, BLOCK_LEN, state_width)
    grad_heads = grad_ssd.reshape(tok_rows, heads_here, head_width).transpose(1, 0, 2)
    grad_heads = grad_heads.reshape(heads_here, blocks, BLOCK_LEN, head_width)
    cumulative = jnp.cumsum(log_decay.reshape(heads_here, blocks, BLOCK_LEN), axis=2)
    block_total = cumulative[..., -1]
    sequence_indices = jnp.arange(BLOCK_LEN)
    upper_mask = sequence_indices[None, :] >= sequence_indices[:, None]
    scores = jnp.einsum("hktn,hksn->hkts", b_heads, c_heads, preferred_element_type=jnp.float32)
    log_gap = cumulative[..., None, :] - cumulative[..., :, None]
    block_weights = jnp.where(upper_mask, scores * jnp.exp(jnp.minimum(log_gap, 0.0)), 0.0).astype(
        jnp.bfloat16
    )
    within = jnp.einsum(
        "hkts,hksp->hktp", block_weights, grad_heads, preferred_element_type=jnp.float32
    )
    grad_float = grad_heads.astype(jnp.float32)
    scaled = (jnp.exp(cumulative)[..., None] * grad_float).astype(jnp.bfloat16)
    block_state = jnp.einsum("hksp,hksn->hkpn", scaled, c_heads, preferred_element_type=jnp.float32)

    def fold_block(carried, inputs):
        state_now, total_now = inputs
        return (state_now + jnp.exp(total_now)[:, None, None] * carried, carried)

    zero_state = jnp.zeros((heads_here, head_width, state_width), jnp.float32)
    summary, inside = lax.scan(
        fold_block, zero_state, (block_state.transpose(1, 0, 2, 3), block_total.T), reverse=True
    )
    decay_total = jnp.exp(jnp.sum(block_total, axis=1))
    tail_decay = jnp.exp(
        jnp.sum(block_total, axis=1, keepdims=True) - jnp.cumsum(block_total, axis=1)
    )

    def combine_pair(earlier, later):
        return (later[0] * earlier[0], later[1] + later[0][:, None, None] * earlier[1])

    identity = (jnp.ones((heads_here,), jnp.float32), zero_state)
    prefix = carried_in((decay_total, summary), SEQ, combine_pair, identity)
    remote = prefix[1]
    full_states = inside.transpose(1, 0, 2, 3) + tail_decay[..., None, None] * remote[:, None]
    carry_low = full_states.astype(jnp.bfloat16)
    across = jnp.einsum("hkpn,hktn->hktp", carry_low, b_heads, preferred_element_type=jnp.float32)
    across = across * jnp.exp(block_total[..., None] - cumulative)[..., None]
    step_sizes = time_step.reshape(heads_here, blocks, BLOCK_LEN)
    grad_head = step_sizes[..., None] * (within + across) + skip[:, None, None, None] * grad_float
    grad_x = (
        grad_head.reshape(heads_here, tok_rows, head_width)
        .transpose(1, 0, 2)
        .reshape(tok_rows, local_width)
    )
    return (grad_x.astype(jnp.bfloat16), grad_gate, grad_out_weight)


def solution(mesh):
    finer = Mesh(mesh.devices.reshape(8, 2, 4, 4), ("seq_0", "seq_1", "head_0", "head_1"))
    return jax.shard_map(
        on_device,
        mesh=finer,
        in_specs=(
            P(SEQ, HEAD),
            P(SEQ, HEAD),
            P(SEQ, HEAD),
            P(SEQ, HEAD),
            P(HEAD),
            P(HEAD, SEQ),
            P(HEAD, SEQ),
            P(SEQ, None, None),
            P(SEQ, None, None),
            P(HEAD),
        ),
        out_specs=(P(SEQ, HEAD), P(SEQ, HEAD), P(SEQ, HEAD)),
        check_vma=False,
    )
```

profile of v0, /device:TPU:2, one launch (start us, length us, event | category | flops | bytes accessed | tf_op | source)
XLA Modules:
  0.0 294.2 jit_solution(11251501523468864543)
XLA Ops:
  8.7 1.3 dynamic-slice.1
  13.3 2.3 reduce-window.6
  16.2 1.5 copy.74
  17.7 2.6 copy.75
  20.4 2.4 all-reduce
  23.1 2.1 convolution_convert_fusion.1
  25.2 29.5 %all-gather.9.cloned.1.call-done = bf16[4096,512]{1,0:T(8,128)(2,1)} async-done(((bf16[256,512]{1,0:T(8,128)(2,1)}), bf16[4096,512]{1,0:T(8,128)(2,1)}) %all-gather.9.cloned.1.call-update) | async-done | bytes 4194320 | tf_op jit(solution)/shard_map/all_gather | solution.py:68
  54.7 82.9 %all-gather.7.cloned.1.call-done = bf16[1024,4096]{1,0:T(8,128)(2,1)} async-done(((bf16[1024,256]{1,0:T(8,128)(2,1)}), bf16[1024,4096]{1,0:T(8,128)(2,1)}) %all-gather.7.cloned.1.call-update) | async-done | bytes 8388624 | tf_op jit(solution)/shard_map/all_gather | solution.py:58
  137.6 11.3 %multiply_reduce_fusion.1 = (f32[1024]{0:T(1024)S(1)}, f32[1024]{0:T(1024)S(1)}, f32[1024,512]{0,1:T(8,128)}) fusion(bf16[1024,512]{0,1:T(8,128)(2,1)S(1)} %copy.74, bf16[1024,512]{0,1:T(8,128)(2,1)} %copy.75, f32[512]{0:T(512)S(1)} %copy-done.7, bf16[1024,4096]{1,0:T(8,128)(2,1)} %all-gather.7.cloned.1.call-done, ...), kind=kOutput, calls=%fused_computation.32 | convolution fusion | flops 4301256704 | bytes 16787456 | tf_op jit(solution)/shard_map/dot_general | solution.py:66
  148.8 8.7 %all-reduce.3 = (f32[1024]{0:T(1024)S(1)}, f32[1024]{0:T(1024)S(1)}) all-reduce(f32[1024]{0:T(1024)S(1)} %get-tuple-element.160, f32[1024]{0:T(1024)S(1)} %get-tuple-element.159), channel_id=1, replica_groups=mesh['seq_0'=8,'seq_1'=2,'head_0'=4,'head_1'=4] {'head_0'}, use_global_device_ids=true, to_apply=%region_6.0 | all-reduce | flops 2048 | bytes 16384 | tf_op jit(solution)/shard_map/psum | solution.py:18
  157.5 10.2 %all-reduce.2 = (f32[1024]{0:T(1024)S(1)}, f32[1024]{0:T(1024)S(1)}) all-reduce(f32[1024]{0:T(1024)S(1)} %get-tuple-element.175, f32[1024]{0:T(1024)S(1)} %get-tuple-element.176), channel_id=1, replica_groups=mesh['seq_0'=8,'seq_1'=2,'head_0'=4,'head_1'=4] {'head_1'}, use_global_device_ids=true, to_apply=%region_7.8 | all-reduce | flops 2048 | bytes 16384 | tf_op jit(solution)/shard_map/psum | solution.py:18
  167.8 4.7 %fusion.9 = (bf16[1024,512]{0,1:T(8,128)(2,1)}, bf16[1024,512]{0,1:T(8,128)(2,1)S(1)}) fusion(bf16[1024,512]{0,1:T(8,128)(2,1)S(1)} %copy.74, bf16[1024,512]{0,1:T(8,128)(2,1)} %copy.75, f32[1024]{0:T(1024)S(1)} %get-tuple-element.173, f32[1024]{0:T(1024)S(1)} %get-tuple-element.182, f32[1024,512]{0,1:T(8,128)} %get-tuple-element.195, f32[512]{0:T(512)S(1)} %copy-done.7, ...), kind=kLoop, calls=%fused_computation.20 | loop fusion | flops 11534336 | bytes 6305792 | tf_op jit(solution)/shard_map/convert_element_type | solution.py:81
  172.5 1.8 fusion.27
  174.3 4.5 %while.17 = (s32[]{:T(128)}, f32[8,64,128]{2,1,0:T(8,128)S(1)}, f32[4,8,64,128]{3,2,1,0:T(8,128)S(1)}, f32[4,8,64,128]{3,2,0,1:T(8,128)}, f32[4,8]{1,0:T(4,128)S(1)}, /*index=5*/s32[]{:T(128)}, s32[]{:T(128)}, s32[]{:T(128)}) while((s32[]{:T(128)}, f32[8,64,128]{2,1,0:T(8,128)S(1)}, f32[4,8,64,128]{3,2,1,0:T(8,128)S(1)}, ...), condition=%wide.region_9.10_spmd.clone, body=%wide.region_8.9_spmd.clone.sunk | while | flops 262148 | bytes 1310944 | solution.py:135
  179.8 2.2 all-gather
  183.0 11.0 %fusion.2 = bf16[4096,512]{0,1:T(8,128)(2,1)} fusion(bf16[1024,4096]{1,0:T(8,128)(2,1)} %all-gather.7.cloned.1.call-done, f32[512]{0:T(512)S(1)} %copy-done.7, bf16[1024,512]{0,1:T(8,128)(2,1)} %copy-done.2, f32[1024]{0:T(1024)S(1)} %get-tuple-element.181, bf16[1024,512]{0,1:T(8,128)(2,1)} %copy.75), kind=kOutput, calls=%fused_computation.7 | convolution fusion | flops 4302307328 | bytes 14686208 | tf_op jit(solution)/shard_map/dot_general | solution.py:85
  194.9 17.7 %all-reduce.1 = f32[64]{0:T(128)S(1)} all-reduce(f32[64]{0:T(128)S(1)} %copy-done.10), channel_id=4, replica_groups=mesh['seq_0'=8,'seq_1'=2,'head_0'=4,'head_1'=4] {'seq_0'}, use_global_device_ids=true, to_apply=%add.1 | all-reduce | flops 64 | bytes 512
  212.7 3.7 %convolution_convert_fusion.2 = bf16[8,1024,128]{2,0,1:T(8,128)(2,1)} fusion(bf16[1024,8,128]{2,1,0:T(8,128)(2,1)} %param.19, s32[8]{0:T(128)S(1)} %and_select_fusion), kind=kOutput, calls=%fused_computation.34 | convolution fusion | flops 17825856 | bytes 4194336 | tf_op jit(solution)/shard_map/tgn,hg->htn/dot_general | solution.py:104
  216.3 2.3 copy.86
  218.6 6.3 %fusion.3 = f32[8,4,256,64]{2,3,1,0:T(8,128)} fusion(f32[8,4,256]{2,1,0:T(4,128)S(1)} %copy.72, pred[256,256]{1,0:T(8,128)(4,1)S(1)} %iota_compare_fusion, bf16[8,4,256,128]{3,0,2,1:T(8,128)(2,1)} %bitcast.136, bf16[8,4,256,128]{3,0,2,1:T(8,128)(2,1)} %bitcast.130, bf16[8,8,4,8,256]{4,3,2,1,0:T(8,128)(2,1)} %bitcast.133), kind=kOutput, calls=%fused_computation.8 | convolution fusion | flops 815792128 | bytes 7438336 | tf_op jit(solution)/shard_map/hkts,hksp->hktp/dot_general | solution.py:123
  224.9 2.1 fusion.53
  227.2 3.3 %fusion.30 = bf16[8,4,8,8,256]{4,3,2,1,0:T(8,128)(2,1)S(1)} fusion(f32[8,4,256,64]{2,3,1,0:T(8,128)} %fusion.3, bf16[8,4,256,128]{3,0,2,1:T(8,128)(2,1)S(1)} %bitcast.131, f32[8]{0:T(128)S(1)} %copy-done.8, f32[8,4,256]{2,1,0:T(4,128)S(1)} %copy.83, f32[8,4,256]{2,1,0:T(4,128)S(1)} %copy.67, bf16[8,8,4,8,256]{4,3,2,1,0:T(8,128)(2,1)} %bitcast.134, ...), kind=kOutput, calls=%fused_computation.42 | convolution fusion | flops 138674176 | bytes 7667872 | tf_op jit(solution)/shard_map/hkpn,hktn->hktp/dot_general | solution.py:151
  230.6 1.3 copy.85
  231.9 53.7 %reduce-scatter.2.cloned.1.call-done = bf16[256,512]{0,1:T(8,128)(2,1)} async-done(((bf16[4096,512]{0,1:T(8,128)(2,1)}), bf16[256,512]{0,1:T(8,128)(2,1)}) %reduce-scatter.2.cloned.1.call-update) | async-done | bytes 262160 | tf_op jit(solution)/shard_map/reduce_scatter | solution.py:84
  (71 shorter events, 14.0 us)
Async XLA Ops:
  7.2 15.9 %copy-start = (bf16[1024,8,128]{2,1,0:T(8,128)(2,1)S(1)}, bf16[1024,8,128]{2,1,0:T(8,128)(2,1)}, u32[]{:S(2)}) copy-start(bf16[1024,8,128]{2,1,0:T(8,128)(2,1)} %param.20) | copy-start | bytes 6291460
  7.2 47.5 %all-gather.9.cloned.1.call-start = ((), (), s32[]{:S(2)}) async-start(), calls=%async_computation.2 | async-start | bytes 4456448 | tf_op jit(solution)/shard_map/all_gather | solution.py:68
  7.9 129.7 %all-gather.7.cloned.1.call-start = ((), (), s32[]{:S(2)}) async-start(), calls=%async_computation.1 | async-start | bytes 8912896 | tf_op jit(solution)/shard_map/all_gather | solution.py:58
  8.7 216.3 %all-gather.11.cloned.1.call-start = ((), (), s32[]{:S(2)}) async-start(), calls=%async_computation.3 | async-start | bytes 2359296 | tf_op jit(solution)/shard_map/all_gather | solution.py:33
  17.7 150.1 %copy-start.2 = (bf16[1024,512]{0,1:T(8,128)(2,1)}, bf16[1024,512]{0,1:T(8,128)(2,1)S(1)}, u32[]{:S(2)}) copy-start(bf16[1024,512]{0,1:T(8,128)(2,1)S(1)} %copy.74) | copy-start | bytes 3145732
  23.1 2.1 copy-start.9
  23.1 114.5 %copy-start.7 = (f32[512]{0:T(512)S(1)}, f32[512]{0:T(512)}, u32[]{:S(2)}) copy-start(f32[512]{0:T(512)} %param.16) | copy-start | bytes 6148
  167.8 4.7 %copy-start.5 = (bf16[8,1024,128]{2,0,1:T(8,128)(2,1)S(1)}, bf16[8,1024,128]{2,0,1:T(8,128)(2,1)}, u32[]{:S(2)}) copy-start(bf16[8,1024,128]{2,0,1:T(8,128)(2,1)} %convolution_convert_fusion.1) | copy-start | bytes 6291460
  172.5 1.8 copy-start.3
  178.8 1.0 copy-start.4
  182.8 102.8 %reduce-scatter.2.cloned.1.call-start = ((), (), s32[]{:S(2)}) async-start(), calls=%async_computation.4 | async-start | bytes 4456448 | tf_op jit(solution)/shard_map/reduce_scatter | solution.py:84
  194.0 0.8 copy-start.6
  194.1 0.8 copy-start.10
  224.9 2.1 copy-start.8
  224.9 2.2 copy-start.1
Sparse Core Ops, SparseCore 0:
  9.8 44.8 all-gather.8
  57.1 80.4 all-gather.6
  182.9 38.5 all-gather.10
  223.9 61.6 reduce-scatter.1
where the time goes:
time: 295 us; the launch traced here: 294 us
  waiting for transfers between devices  167 us (57%)
  blocking collectives  41.2 us (14%)
  matrix products  39.5 us (13%)
  other arithmetic  15.8 us (5%)
  between operations  15.3 us (5%)
  local copies, waits for them, and re-layouts  14.4 us (5%)
    all_gather x1, waiting for transfers between devices, on_device(): full_grad = lax.all_gather(grad_output, HEAD, axis=1, tiled=True)  82.9 us
    reduce_scatter x1, waiting for transfers between devices, on_device(): lax.psum_scatter(lax.dot_general(columns, normed, (((0,), (0,)), ((), ())...  53.7 us
    all_gather x1, waiting for transfers between devices, on_device(): lax.all_gather(out_weight, SEQ, axis=0, tiled=True)  29.5 us
    unnamed x2, blocking collectives  20.1 us
    psum x2, blocking collectives, over_axes(): x = lax.psum(x, axis)  18.9 us
    unnamed x32, local copies, waits for them, and re-layouts  13.2 us
    dot_general x1, matrix products, on_device(): jnp.dot(columns, lax.all_gather(out_weight, SEQ, axis=0, tiled=True), pre...  11.3 us
    dot_general x1, matrix products, on_device(): lax.dot_general(columns, normed, (((0,), (0,)), ((), ())), preferred_elem...  11 us
  transfers between devices with their start and end apart: 4, of which 3 were waited for; matrix products, arithmetic and copies ran while one was open for 15% of the time, Pallas kernels for 0%

commit v1 on v0

--- a/solution.py
+++ b/solution.py
@@ -11,11 +11,12 @@
 HEAD = ("head_0", "head_1")
 SEQ = ("seq_0", "seq_1")
 epsilon = 1e-05
+_settle_modes = lambda vec, which_axis: lax.all_gather(vec, which_axis).sum(axis=0)
 
 
 def over_axes(x, axes):
     for axis in axes:
-        x = lax.psum(x, axis)
+        x = _settle_modes(x, axis)
     return x
 
 

time: 295 us -> 326 us (1.11)
  blocking collectives: 41.2 us -> 70.2 us
    all_gather x0 -> x4, blocking collectives: none -> 48.1 us  [lax.all_gather(vec, which_axis).sum(axis=0)]
    psum x2 -> x0, blocking collectives: 18.9 us -> none  [over_axes(): x = lax.psum(x, axis)]
    unnamed x32 -> x48, local copies, waits for them, and re-layouts: 13.2 us -> 13.2 us
  transfers between devices with their start and end apart: 4 -> 4, of which waited for: 3 -> 3; matrix products, arithmetic and copies ran while one was open for 15% -> 13% of each run, Pallas kernels for 0% -> 0%
where the time goes in v1:
time: 326 us; the launch traced here: 325 us
  waiting for transfers between devices  169 us (52%)
  blocking collectives  70.2 us (22%)
  matrix products  39.5 us (12%)
  other arithmetic  16.3 us (5%)
  between operations  15.4 us (5%)
  local copies, waits for them, and re-layouts  14.5 us (4%)
    all_gather x1, waiting for transfers between devices, on_device(): full_grad = lax.all_gather(grad_output, HEAD, axis=1, tiled=True)  82.9 us
    reduce_scatter x1, waiting for transfers between devices, on_device(): lax.psum_scatter(lax.dot_general(columns, normed, (((0,), (0,)), ((), ())...  55.4 us
    all_gather x4, blocking collectives, lax.all_gather(vec, which_axis).sum(axis=0)  48.1 us
    all_gather x1, waiting for transfers between devices, on_device(): lax.all_gather(out_weight, SEQ, axis=0, tiled=True)  29 us
    unnamed x2, blocking collectives  20 us
    unnamed x48, local copies, waits for them, and re-layouts  13.2 us
    dot_general x1, matrix products, on_device(): jnp.dot(columns, lax.all_gather(out_weight, SEQ, axis=0, tiled=True), pre...  11.3 us
    dot_general x1, matrix products, on_device(): lax.dot_general(columns, normed, (((0,), (0,)), ((), ())), preferred_elem...  11 us
  transfers between devices with their start and end apart: 4, of which 3 were waited for; matrix products, arithmetic and copies ran while one was open for 13% of the time, Pallas kernels for 0%

profile of v1, /device:TPU:2, one launch (start us, length us, event | category | flops | bytes accessed | tf_op | source)
XLA Modules:
  0.0 325.1 jit_solution(12308254657206856414)
XLA Ops:
  13.3 2.3 reduce-window.6
  16.2 1.5 copy.95
  17.7 2.6 copy.96
  20.4 2.4 all-reduce
  23.6 2.1 convolution_convert_fusion.1
  25.7 29.0 %all-gather.13.cloned.1.call-done = bf16[4096,512]{1,0:T(8,128)(2,1)} async-done(((bf16[256,512]{1,0:T(8,128)(2,1)}), bf16[4096,512]{1,0:T(8,128)(2,1)}) %all-gather.13.cloned.1.call-update) | async-done | bytes 4194320 | tf_op jit(solution)/shard_map/all_gather | solution.py:69
  54.7 82.9 %all-gather.11.cloned.1.call-done = bf16[1024,4096]{1,0:T(8,128)(2,1)} async-done(((bf16[1024,256]{1,0:T(8,128)(2,1)}), bf16[1024,4096]{1,0:T(8,128)(2,1)}) %all-gather.11.cloned.1.call-update) | async-done | bytes 8388624 | tf_op jit(solution)/shard_map/all_gather | solution.py:59
  137.6 11.3 %multiply_reduce_fusion.1 = (f32[1024]{0:T(1024)S(1)}, f32[1024]{0:T(1024)S(1)}, f32[1024,512]{0,1:T(8,128)}) fusion(bf16[1024,512]{0,1:T(8,128)(2,1)S(1)} %copy.95, bf16[1024,512]{0,1:T(8,128)(2,1)} %copy.96, f32[512]{0:T(512)S(1)} %copy-done.9, bf16[1024,4096]{1,0:T(8,128)(2,1)} %all-gather.11.cloned.1.call-done, ...), kind=kOutput, calls=%fused_computation.32 | convolution fusion | flops 4301256704 | bytes 16787456 | tf_op jit(solution)/shard_map/dot_general | solution.py:67
  148.8 12.0 %all-gather = f32[4096]{0:T(1024)S(1)} all-gather(f32[1024]{0:T(1024)S(1)} %get-tuple-element.167), channel_id=2, replica_groups=mesh['seq_0'=8,'seq_1'=2,'head_0'=4,'head_1'=4] {'head_0'}, dimensions={0}, use_global_device_ids=true | all-gather | bytes 20480 | tf_op jit(solution)/shard_map/all_gather | solution.py:14
  160.9 12.0 %all-gather.1 = f32[4096]{0:T(1024)S(1)} all-gather(f32[1024]{0:T(1024)S(1)} %reduce_sum.68), channel_id=3, replica_groups=mesh['seq_0'=8,'seq_1'=2,'head_0'=4,'head_1'=4] {'head_1'}, dimensions={0}, use_global_device_ids=true | all-gather | bytes 20480 | tf_op jit(solution)/shard_map/all_gather | solution.py:14
  173.0 12.0 %all-gather.2 = f32[4096]{0:T(1024)S(1)} all-gather(f32[1024]{0:T(1024)S(1)} %get-tuple-element.168), channel_id=4, replica_groups=mesh['seq_0'=8,'seq_1'=2,'head_0'=4,'head_1'=4] {'head_0'}, dimensions={0}, use_global_device_ids=true | all-gather | bytes 20480 | tf_op jit(solution)/shard_map/all_gather | solution.py:14
  185.0 12.0 %all-gather.3 = f32[4096]{0:T(1024)S(1)} all-gather(f32[1024]{0:T(1024)S(1)} %reduce_sum.71), channel_id=5, replica_groups=mesh['seq_0'=8,'seq_1'=2,'head_0'=4,'head_1'=4] {'head_1'}, dimensions={0}, use_global_device_ids=true | all-gather | bytes 20480 | tf_op jit(solution)/shard_map/all_gather | solution.py:14
  197.1 4.6 %fusion.9 = (bf16[1024,512]{0,1:T(8,128)(2,1)}, bf16[1024,512]{0,1:T(8,128)(2,1)S(1)}) fusion(bf16[1024,512]{0,1:T(8,128)(2,1)S(1)} %copy.95, bf16[1024,512]{0,1:T(8,128)(2,1)} %copy.96, f32[1024]{0:T(1024)S(1)} %reduce_sum.72, f32[1024]{0:T(1024)S(1)} %get-tuple-element.186, f32[1024,512]{0,1:T(8,128)} %get-tuple-element.199, f32[512]{0:T(512)} %param.16, ...), kind=kLoop, calls=%fused_computation.20 | loop fusion | flops 11534336 | bytes 6305792 | tf_op jit(solution)/shard_map/convert_element_type | solution.py:82
  201.7 1.8 fusion.27
  203.6 4.5 %while.17 = (s32[]{:T(128)}, f32[8,64,128]{2,1,0:T(8,128)S(1)}, f32[4,8,64,128]{3,2,1,0:T(8,128)S(1)}, f32[4,8,64,128]{3,2,0,1:T(8,128)}, f32[4,8]{1,0:T(4,128)S(1)}, /*index=5*/s32[]{:T(128)}, s32[]{:T(128)}, s32[]{:T(128)}) while((s32[]{:T(128)}, f32[8,64,128]{2,1,0:T(8,128)S(1)}, f32[4,8,64,128]{3,2,1,0:T(8,128)S(1)}, ...), condition=%wide.region_9.10_spmd.clone, body=%wide.region_8.9_spmd.clone.sunk | while | flops 262148 | bytes 1310944 | solution.py:136
  209.1 2.2 all-gather.4
  212.4 11.0 %fusion.2 = bf16[4096,512]{0,1:T(8,128)(2,1)} fusion(bf16[1024,4096]{1,0:T(8,128)(2,1)} %all-gather.11.cloned.1.call-done, f32[512]{0:T(512)S(1)} %copy-done.10, bf16[1024,512]{0,1:T(8,128)(2,1)} %copy-done.2, f32[1024]{0:T(1024)S(1)} %get-tuple-element.185, bf16[1024,512]{0,1:T(8,128)(2,1)} %copy.96), kind=kOutput, calls=%fused_computation.7 | convolution fusion | flops 4302307328 | bytes 14686208 | tf_op jit(solution)/shard_map/dot_general | solution.py:86
  224.2 17.5 %all-reduce.1 = f32[64]{0:T(128)S(1)} all-reduce(f32[64]{0:T(128)S(1)} %copy-done.18), channel_id=8, replica_groups=mesh['seq_0'=8,'seq_1'=2,'head_0'=4,'head_1'=4] {'seq_0'}, use_global_device_ids=true, to_apply=%add.1 | all-reduce | flops 64 | bytes 512
  241.8 3.7 %convolution_convert_fusion.2 = bf16[8,1024,128]{2,0,1:T(8,128)(2,1)} fusion(bf16[1024,8,128]{2,1,0:T(8,128)(2,1)} %param.19, s32[8]{0:T(128)S(1)} %copy-done.12), kind=kOutput, calls=%fused_computation.34 | convolution fusion | flops 17825856 | bytes 4194336 | tf_op jit(solution)/shard_map/tgn,hg->htn/dot_general | solution.py:105
  245.5 2.3 copy.107
  247.8 6.4 %fusion.3 = f32[8,4,256,64]{2,3,1,0:T(8,128)} fusion(f32[8,4,256]{2,1,0:T(4,128)S(1)} %copy.93, pred[256,256]{1,0:T(8,128)(4,1)S(1)} %iota_compare_fusion, bf16[8,4,256,128]{3,0,2,1:T(8,128)(2,1)} %bitcast.136, bf16[8,4,256,128]{3,0,2,1:T(8,128)(2,1)} %bitcast.130, bf16[8,8,4,8,256]{4,3,2,1,0:T(8,128)(2,1)} %bitcast.133), kind=kOutput, calls=%fused_computation.8 | convolution fusion | flops 815792128 | bytes 7438336 | tf_op jit(solution)/shard_map/hkts,hksp->hktp/dot_general | solution.py:124
  254.1 2.1 fusion.53
  256.4 3.3 %fusion.30 = bf16[8,4,8,8,256]{4,3,2,1,0:T(8,128)(2,1)S(1)} fusion(f32[8,4,256,64]{2,3,1,0:T(8,128)} %fusion.3, bf16[8,4,256,128]{3,0,2,1:T(8,128)(2,1)S(1)} %bitcast.131, f32[8]{0:T(128)S(1)} %copy-done.16, f32[8,4,256]{2,1,0:T(4,128)S(1)} %copy.104, f32[8,4,256]{2,1,0:T(4,128)S(1)} %copy.88, bf16[8,8,4,8,256]{4,3,2,1,0:T(8,128)(2,1)} %bitcast.134, ...), kind=kOutput, calls=%fused_computation.42 | convolution fusion | flops 138674176 | bytes 7667872 | tf_op jit(solution)/shard_map/hkpn,hktn->hktp/dot_general | solution.py:152
  261.1 55.4 %reduce-scatter.2.cloned.1.call-done = bf16[256,512]{0,1:T(8,128)(2,1)} async-done(((bf16[4096,512]{0,1:T(8,128)(2,1)}), bf16[256,512]{0,1:T(8,128)(2,1)}) %reduce-scatter.2.cloned.1.call-update) | async-done | bytes 262160 | tf_op jit(solution)/shard_map/reduce_scatter | solution.py:85
  (97 shorter events, 17.2 us)
Async XLA Ops:
  7.2 16.4 %copy-start = (bf16[1024,8,128]{2,1,0:T(8,128)(2,1)S(1)}, bf16[1024,8,128]{2,1,0:T(8,128)(2,1)}, u32[]{:S(2)}) copy-start(bf16[1024,8,128]{2,1,0:T(8,128)(2,1)} %param.20) | copy-start | bytes 6291460
  7.2 47.5 %all-gather.13.cloned.1.call-start = ((), (), s32[]{:S(2)}) async-start(), calls=%async_computation.2 | async-start | bytes 4456448 | tf_op jit(solution)/shard_map/all_gather | solution.py:69
  7.9 129.7 %all-gather.11.cloned.1.call-start = ((), (), s32[]{:S(2)}) async-start(), calls=%async_computation.1 | async-start | bytes 8912896 | tf_op jit(solution)/shard_map/all_gather | solution.py:59
  8.7 245.5 %all-gather.15.cloned.1.call-start = ((), (), s32[]{:S(2)}) async-start(), calls=%async_computation.3 | async-start | bytes 2359296 | tf_op jit(solution)/shard_map/all_gather | solution.py:34
  16.1 4.3 %copy-start.13 = (f32[8]{0:T(128)}, f32[8]{0:T(128)S(1)}, u32[]{:S(2)}) copy-start(f32[8]{0:T(128)S(1)} %get-tuple-element.169) | copy-start | bytes 100
  17.7 179.4 %copy-start.2 = (bf16[1024,512]{0,1:T(8,128)(2,1)}, bf16[1024,512]{0,1:T(8,128)(2,1)S(1)}, u32[]{:S(2)}) copy-start(bf16[1024,512]{0,1:T(8,128)(2,1)S(1)} %copy.95) | copy-start | bytes 3145732
  22.9 2.8 copy-start.11
  23.6 2.1 copy-start.17
  23.6 114.0 %copy-start.9 = (f32[512]{0:T(512)S(1)}, f32[512]{0:T(512)}, u32[]{:S(2)}) copy-start(f32[512]{0:T(512)} %param.16) | copy-start | bytes 6148
  197.1 4.6 %copy-start.5 = (bf16[8,1024,128]{2,0,1:T(8,128)(2,1)S(1)}, bf16[8,1024,128]{2,0,1:T(8,128)(2,1)}, u32[]{:S(2)}) copy-start(bf16[8,1024,128]{2,0,1:T(8,128)(2,1)} %convolution_convert_fusion.1) | copy-start | bytes 6291460
  201.7 1.8 copy-start.3
  203.6 7.7 %copy-start.7 = (f32[8]{0:T(128)S(1)}, f32[8]{0:T(128)}, u32[]{:S(2)}) copy-start(f32[8]{0:T(128)} %get-tuple-element.188) | copy-start | bytes 100
  203.6 7.7 %copy-start.8 = (f32[8]{0:T(128)S(1)}, f32[8]{0:T(128)}, u32[]{:S(2)}) copy-start(f32[8]{0:T(128)} %get-tuple-element.190) | copy-start | bytes 100
  203.6 8.7 %copy-start.10 = (f32[512]{0:T(512)S(1)}, f32[512]{0:T(512)}, u32[]{:S(2)}) copy-start(f32[512]{0:T(512)} %param.16) | copy-start | bytes 6148
  208.1 1.0 copy-start.4
  212.1 104.4 %reduce-scatter.2.cloned.1.call-start = ((), (), s32[]{:S(2)}) async-start(), calls=%async_computation.4 | async-start | bytes 4456448 | tf_op jit(solution)/shard_map/reduce_scatter | solution.py:85
  223.4 0.8 copy-start.6
  223.4 0.8 copy-start.18
  223.4 18.4 %copy-start.14 = (f32[8]{0:T(128)S(1)}, f32[8]{0:T(128)}, u32[]{:S(2)}) copy-start(f32[8]{0:T(128)} %copy-done.13) | copy-start | bytes 100
  223.4 18.4 %copy-start.12 = (s32[8]{0:T(128)S(1)}, s32[8]{0:T(128)}, u32[]{:S(2)}) copy-start(s32[8]{0:T(128)} %copy-done.11) | copy-start | bytes 100
  247.8 6.4 %copy-start.15 = (f32[8]{0:T(128)S(1)}, f32[8]{0:T(128)}, u32[]{:S(2)}) copy-start(f32[8]{0:T(128)} %get-tuple-element.187) | copy-start | bytes 100
  254.1 2.1 copy-start.16
  254.1 2.2 copy-start.1
Sparse Core Ops, SparseCore 0:
  9.8 44.8 all-gather.12
  57.1 80.4 all-gather.10
  212.2 40.4 all-gather.14
  255.2 61.3 reduce-scatter.1
